TPU v7x, 512 devices: a whole 4x8x8 slice. The times are simulated.
512 devices in a mesh: dp: 16 (over z, core), fsdp: 32 (over x, y).
Axes of the slice: x: 4, y: 8, z: 8, core: 2. Of those that a mesh axis runs over, the one named last changes fastest.
Arguments:
- passages: bfloat16 [16, 32, 40, 8, 2048], P('dp', 'fsdp'), may hold values from -6 to 6
- counts: int32 [16, 32], P('dp', 'fsdp'), may hold values from 1 to 40, as said below
- helper_table: int32 [16, 32, 2, 32], P('dp', 'fsdp'), may hold values from -1 to 31, as said below
- norm_gain: float32 [2048], replicated, may hold values from 0.1 to 1.9
- projection: bfloat16 [2048, 2048], P('fsdp'), may hold values from -0.125 to 0.125
- queries: bfloat16 [16, 32, 16, 1024], P('dp', 'fsdp'), may hold values from -140 to 140
- cotangent: bfloat16 [16, 32, 24, 8, 2048], P('dp', 'fsdp'), may hold values from -0.0234375 to 0.0234375
Outputs:
- context: bfloat16 [16, 32, 16, 1024], P('dp', 'fsdp')
- gain_gradient: float32 [2048], P('fsdp')
Inputs may be any that keep to these rules, and one draw needn't show every extreme that they name: `counts`: A question with passages beyond the first 8 has 8 plus that many; some question of every group has 40. `helper_table`: entries at e are -1 exactly when 8 + e is not below the question's count; otherwise row 0 names a device of the same group and row 1 a slot from 0 to 15. No two passages of a group share a device and slot; some device of every group has all 16 slots taken; one question sends at most 1 passages to one device, and some question of every group sends exactly that many to some device.
All inputs are finite; a program needn't handle non-finite values.
Results may differ from a plain program's by a relative error of at most 0.0095.
The roundings to bfloat16 on the way count: a program that leaves them out, or rounds other values in their place, can miss the bound.
Values may be sent and summed in bfloat16 or wider, within the bound.
No kernel may reach another device: no remote copies, remote signals or barrier semaphores. Data moves between devices by JAX's collectives and lax.ppermute only.
A program may use at most 64 MiB of HBM per device.

v0:
```python
import jax
import jax.numpy as jnp
from jax import lax
from jax.sharding import Mesh
from jax.sharding import PartitionSpec as P

D = 2048
HEADS = 32
HEAD_DIM = 32
HW = 1024
DEC = 16
LEN = 8
PMAX = 40
KEEP = 8
HELP = 16
ENC = 24
DP = ("dp_0", "dp_1")
EPSILON = 1e-06


def cut_along(array, dim, peers):
    dims = array.shape
    parts = array.reshape(*dims[:dim], peers, dims[dim] // peers, *dims[dim + 1 :])
    return jnp.moveaxis(parts, dim, 0)


def sent_and_summed(array, axis, dim):
    peers = lax.axis_size(axis)
    parts = lax.all_to_all(cut_along(array, dim, peers), axis, 0, 0, tiled=True)
    return jnp.sum(parts, axis=0)


def by_axis(array, axes):
    for axis in axes:
        array = lax.psum(array, axis)
    return array


def normalize(states):
    values = states.astype(jnp.float32)
    scaling = lax.rsqrt(jnp.mean(values * values, axis=-1, keepdims=True) + EPSILON)
    return values * scaling


def rank_slots(helpers, alive_mask, peer_count, per_peer):
    onehot = (
        (helpers[:, None] == lax.iota(jnp.int32, peer_count)[None, :]) & alive_mask[:, None]
    ).astype(jnp.int32)
    before = jnp.cumsum(onehot, axis=0) - onehot
    ranking = jnp.sum(before * onehot, axis=1)
    target = helpers * per_peer + ranking
    places = lax.iota(jnp.int32, peer_count * per_peer)
    return (places[:, None] == target[None, :]) & alive_mask[None, :]


def shards(passages, counts, helper_table, norm_gain, projection, queries, cotangent):
    peer_count = lax.axis_size("fsdp")
    spare_slots = PMAX - KEEP
    per_peer = -(-spare_slots // peer_count)
    stored = passages.reshape(PMAX, LEN, D)
    passage_count = counts.reshape(())
    table_rows = helper_table.reshape(2, spare_slots)
    alive_mask = table_rows[0] >= 0
    selector = rank_slots(table_rows[0], alive_mask, peer_count, per_peer)
    select_matrix = selector.astype(jnp.bfloat16)
    outgoing = jnp.dot(
        select_matrix,
        stored[KEEP:].reshape(spare_slots, LEN * D),
        preferred_element_type=jnp.float32,
    ).astype(jnp.bfloat16)
    slot_tags = jnp.sum(jnp.where(selector, table_rows[1][None, :] + 1, 0), axis=1) - 1
    arrived, arrived_tags = (
        lax.all_to_all(
            outgoing.reshape(peer_count, per_peer, LEN * D),
            "fsdp",
            split_axis=0,
            concat_axis=0,
            tiled=True,
        ),
        lax.all_to_all(
            slot_tags.reshape(peer_count, per_peer), "fsdp", split_axis=0, concat_axis=0, tiled=True
        ),
    )
    pick_matrix = arrived_tags.reshape(-1)[None, :] == lax.iota(jnp.int32, HELP)[:, None]
    helped = jnp.dot(
        pick_matrix.astype(jnp.bfloat16),
        arrived.reshape(-1, LEN * D),
        preferred_element_type=jnp.float32,
    ).astype(jnp.bfloat16)
    encoded = jnp.concatenate([stored[:KEEP], helped.reshape(HELP, LEN, D)], axis=0)
    normal = normalize(encoded).reshape(ENC * LEN, D)
    scaled = (normal * norm_gain).astype(jnp.bfloat16)
    slot_alive = jnp.concatenate(
        [lax.iota(jnp.int32, KEEP) < passage_count, jnp.any(pick_matrix, axis=1)]
    )
    token_alive = jnp.repeat(slot_alive, LEN).astype(jnp.float32)
    upstream = cotangent.reshape(ENC * LEN, 2 * HW)
    weight_piece = lax.all_gather(projection, "fsdp", axis=0, tiled=True)
    partial_states = jnp.dot(scaled, weight_piece, preferred_element_type=jnp.float32)
    back_piece = lax.dot_general(
        upstream, weight_piece, (((1,), (1,)), ((), ())), preferred_element_type=jnp.float32
    )
    row_terms = jnp.dot(token_alive, normal * back_piece, precision=lax.Precision.HIGHEST)
    state_rows = partial_states.astype(jnp.bfloat16).reshape(ENC, LEN * 2 * HW)
    returning = jnp.dot(
        pick_matrix.T.astype(jnp.bfloat16), state_rows[KEEP:], preferred_element_type=jnp.float32
    ).astype(jnp.bfloat16)
    returned = lax.all_to_all(
        returning.reshape(peer_count, per_peer, LEN * 2 * HW),
        "fsdp",
        split_axis=0,
        concat_axis=0,
        tiled=True,
    )
    remote_states = jnp.dot(
        select_matrix.T, returned.reshape(-1, LEN * 2 * HW), preferred_element_type=jnp.float32
    ).astype(jnp.bfloat16)
    all_states = jnp.concatenate([state_rows[:KEEP], remote_states], axis=0).reshape(
        PMAX * LEN, 2, HEADS, HEAD_DIM
    )
    key_rows = all_states[:, 0]
    value_rows = all_states[:, 1]
    query_rows = queries.reshape(DEC, HEADS, HEAD_DIM)
    scores = jnp.einsum(
        "qhd,thd->hqt", query_rows, key_rows, preferred_element_type=jnp.float32
    ) * HEAD_DIM ** (-0.5)
    token_live = jnp.repeat(lax.iota(jnp.int32, PMAX) < passage_count, LEN)
    scores = jnp.where(token_live[None, None, :], scores, -jnp.inf)
    highest = jnp.max(scores, axis=-1, keepdims=True)
    raised = jnp.exp(scores - highest)
    weights = (raised / jnp.sum(raised, axis=-1, keepdims=True)).astype(jnp.bfloat16)
    context = jnp.einsum("hqt,thd->qhd", weights, value_rows, preferred_element_type=jnp.float32)
    context_out = context.astype(jnp.bfloat16).reshape(1, 1, DEC, HW)
    group_share = sent_and_summed(row_terms, "fsdp", 0)
    gradient = by_axis(group_share, DP)
    return (context_out, gradient)


def solution(mesh):
    split = Mesh(mesh.devices.reshape(8, 2, mesh.shape["fsdp"]), ("dp_0", "dp_1", "fsdp"))
    return jax.shard_map(
        shards,
        mesh=split,
        in_specs=(
            P(DP, "fsdp", None, None, None),
            P(DP, "fsdp"),
            P(DP, "fsdp", None, None),
            P(),
            P("fsdp", None),
            P(DP, "fsdp", None, None),
            P(DP, "fsdp", None, None, None),
        ),
        out_specs=(P(DP, "fsdp", None, None), P("fsdp")),
        check_vma=False,
    )
```

profile of v0, /device:TPU:8, one launch (start us, length us, event | category | flops | bytes accessed | tf_op | source)
XLA Modules:
  0.0 233.3 jit_solution(2594520575006294680)
XLA Ops:
  7.2 0.0 copy-start
  7.2 0.0 all-gather.2.cloned.1.call-start
  7.2 0.7 all-gather.2.cloned.1.call-update
  7.9 0.7 broadcast_compare_fusion
  8.6 0.8 add_bitcast_fusion.1
  9.4 0.1 fusion.29
  9.4 0.1 reduce_window_sum.11
  9.5 0.2 select_reduce_fusion.1
  9.7 0.7 fusion.39
  10.4 0.1 select_reduce_fusion
  10.5 0.7 copy.33
  11.2 10.2 %all-to-all-start = ((s32[32,1,1]{2,1,0:T(1,128)}), s32[32,1,1]{2,1,0:T(1,128)S(1)}, u32[]{:S(2)}, u32[]{:S(2)}) async-start(s32[32,1,1]{2,1,0:T(1,128)} %copy.33), calls=%async_computation | async-start | bytes 32768 | tf_op jit(solution)/shard_map/all_to_all | solution.py:80
  21.4 0.6 copy.46
  22.0 0.4 fusion.1
  22.4 0.5 broadcast.61
  22.9 1.4 reduce.2
  24.4 1.6 reshape.139
  26.0 4.0 %all-to-all-done = s32[32,1,1]{2,1,0:T(1,128)S(1)} async-done(((s32[32,1,1]{2,1,0:T(1,128)}), s32[32,1,1]{2,1,0:T(1,128)S(1)}, u32[]{:S(2)}, u32[]{:S(2)}) %all-to-all-start) | async-done | bytes 160 | tf_op jit(solution)/shard_map/all_to_all | solution.py:80
  29.9 5.9 %all-to-all-start.1 = ((bf16[32,2,8192]{2,1,0:T(2,128)(2,1)}), bf16[32,2,8192]{2,1,0:T(2,128)(2,1)}, u32[]{:S(2)}, u32[]{:S(2)}) async-start(bf16[32,2,8192]{2,1,0:T(2,128)(2,1)} %reshape.139), calls=%async_computation.1 | async-start | bytes 2097152 | tf_op jit(solution)/shard_map/all_to_all | solution.py:73
  36.5 0.7 reduce.1
  37.2 0.1 fusion.30
  37.3 0.1 pad_add_fusion
  37.4 0.1 broadcast_in_dim.45
  37.5 0.1 reshape.135
  37.6 33.8 %all-to-all-done.1 = bf16[32,2,8192]{2,1,0:T(2,128)(2,1)} async-done(((bf16[32,2,8192]{2,1,0:T(2,128)(2,1)}), bf16[32,2,8192]{2,1,0:T(2,128)(2,1)}, u32[]{:S(2)}, u32[]{:S(2)}) %all-to-all-start.1) | async-done | bytes 1048608 | tf_op jit(solution)/shard_map/all_to_all | solution.py:73
  71.4 4.3 %reshape.140 = bf16[32,1,16384]{2,1,0:T(2,128)(2,1)S(1)} reshape(bf16[32,2,8192]{2,1,0:T(2,128)(2,1)} %all-to-all-done.1) | data formatting | bytes 2097152
  75.7 1.2 convolution_convert_fusion.3
  77.0 0.3 copy.47
  77.3 0.2 fusion.7
  77.5 0.1 rsqrt.12
  77.6 51.0 %all-gather.2.cloned.1.call-done = bf16[2048,2048]{1,0:T(8,128)(2,1)} async-done(((bf16[64,2048]{1,0:T(8,128)(2,1)}), bf16[2048,2048]{1,0:T(8,128)(2,1)}) %all-gather.2.cloned.1.call-update) | async-done | bytes 8388624 | tf_op jit(solution)/shard_map/all_gather | solution.py:98
  128.6 5.2 %convolution_convert_fusion.4 = bf16[192,2048]{1,0:T(8,128)(2,1)S(1)} fusion(bf16[2048,2048]{1,0:T(8,128)(2,1)} %all-gather.2.cloned.1.call-done, f32[2048]{0:T(1024)S(1)} %copy-done.12, f32[192]{0:T(256)S(1)} %rsqrt.12, bf16[16,8,2048]{2,1,0:T(8,128)(2,1)S(1)} %bitcast.75, bf16[8,8,2048]{2,1,0:T(8,128)(2,1)S(1)} %slice_bitcast_fusion), kind=kOutput, calls=%fused_computation.9 | convolution fusion | flops 1612972032 | bytes 9970432 | tf_op jit(solution)/shard_map/dot_general | solution.py:99
  133.9 0.2 slice.45
  134.2 0.6 copy-done.5
  134.8 0.2 copy-done.4
  135.0 7.4 %fusion.3 = f32[2048,192]{0,1:T(8,128)} fusion(bf16[2048,2048]{1,0:T(8,128)(2,1)} %all-gather.2.cloned.1.call-done, bf16[1,1,24,8,2048]{4,3,2,1,0:T(8,128)(2,1)S(1)} %copy-done, f32[192]{0:T(256)S(1)} %rsqrt.12, bf16[16,8,2048]{2,1,0:T(8,128)(2,1)S(1)} %bitcast.76, bf16[8,8,2048]{2,1,0:T(8,128)(2,1)S(1)} %copy-done.4), kind=kOutput, calls=%fused_computation.8 | convolution fusion | flops 1612185600 | bytes 11535104 | tf_op jit(solution)/shard_map/dot_general | solution.py:100
  142.4 1.8 copy.40
  144.3 2.0 convolution_bitcast_fusion
  146.3 7.4 %all-to-all-start.3 = ((f32[32,1,64]{2,1,0:T(1,128)}), f32[32,1,64]{2,1,0:T(1,128)S(1)}, u32[]{:S(2)}, u32[]{:S(2)}) async-start(f32[32,1,64]{2,1,0:T(1,128)} %convolution_bitcast_fusion), calls=%async_computation.3 | async-start | bytes 32768 | tf_op jit(solution)/shard_map/all_to_all | solution.py:29
  153.7 0.5 fusion.2
  154.1 1.4 reduce.3
  155.6 1.6 reshape.141
  157.2 5.0 %all-to-all-done.3 = f32[32,1,64]{2,1,0:T(1,128)S(1)} async-done(((f32[32,1,64]{2,1,0:T(1,128)}), f32[32,1,64]{2,1,0:T(1,128)S(1)}, u32[]{:S(2)}, u32[]{:S(2)}) %all-to-all-start.3) | async-done | bytes 8224 | tf_op jit(solution)/shard_map/all_to_all | solution.py:29
  162.2 5.7 %all-to-all-start.2 = ((bf16[32,2,8192]{2,1,0:T(2,128)(2,1)}), bf16[32,2,8192]{2,1,0:T(2,128)(2,1)}, u32[]{:S(2)}, u32[]{:S(2)}) async-start(bf16[32,2,8192]{2,1,0:T(2,128)(2,1)} %reshape.141), calls=%async_computation.2 | async-start | bytes 2097152 | tf_op jit(solution)/shard_map/all_to_all | solution.py:108
  167.9 0.1 broadcast_in_dim.41
  168.0 0.6 broadcast_in_dim.42
  168.6 0.1 reshape.130
  168.8 0.1 slice.43
  168.9 0.1 reduce_sum.49
  169.0 18.1 %psum.14 = f32[64]{0:T(128)S(1)} all-reduce(f32[64]{0:T(128)S(1)} %reduce_sum.49), channel_id=1, replica_groups=mesh['dp_0'=8,'dp_1'=2,'fsdp'=32] {'dp_0'}, use_global_device_ids=true, to_apply=%region_8.9 | all-reduce | flops 64 | bytes 512 | tf_op jit(solution)/shard_map/psum | solution.py:35
  187.1 3.0 %psum.15 = f32[64]{0:T(128)} all-reduce(f32[64]{0:T(128)S(1)} %psum.14), channel_id=1, replica_groups=mesh['dp_0'=8,'dp_1'=2,'fsdp'=32] {'dp_1'}, use_global_device_ids=true, to_apply=%region_9.10 | all-reduce | flops 64 | bytes 512 | tf_op jit(solution)/shard_map/psum | solution.py:35
  190.1 4.8 %all-to-all-done.2 = bf16[32,2,8192]{2,1,0:T(2,128)(2,1)} async-done(((bf16[32,2,8192]{2,1,0:T(2,128)(2,1)}), bf16[32,2,8192]{2,1,0:T(2,128)(2,1)}, u32[]{:S(2)}, u32[]{:S(2)}) %all-to-all-start.2) | async-done | bytes 1048608 | tf_op jit(solution)/shard_map/all_to_all | solution.py:108
  194.9 4.3 %reshape.142 = bf16[32,1,16384]{2,1,0:T(2,128)(2,1)S(1)} reshape(bf16[32,2,8192]{2,1,0:T(2,128)(2,1)} %all-to-all-done.2) | data formatting | bytes 2097152
  199.2 1.4 convolution_convert_fusion
  200.7 0.1 pad_maximum_fusion
  200.8 5.4 %reshape.128 = bf16[320,2,32,32]{3,2,1,0:T(8,128)(2,1)} reshape(bf16[40,16384]{1,0:T(8,128)(2,1)S(1)} %pad_maximum_fusion) | data formatting | bytes 2621440 | tf_op jit(solution)/shard_map/reshape | solution.py:118
  206.2 5.0 %fusion.40 = (bf16[320,1,32,32]{3,2,1,0:T(8,128)(2,1)}, bf16[320,1,32,32]{3,2,1,0:T(8,128)(2,1)S(1)}) fusion(bf16[320,2,32,32]{3,2,1,0:T(8,128)(2,1)} %reshape.128), kind=kLoop, calls=%fused_computation.65 | loop fusion | bytes 2621440 | tf_op jit(solution)/shard_map/slice | solution.py:121
  211.2 5.1 %copy.45 = bf16[320,1,32,32]{0,3,2,1:T(8,128)(2,1)} copy(bf16[320,1,32,32]{3,2,1,0:T(8,128)(2,1)} %get-tuple-element.2) | data formatting | bytes 1310720
  216.2 1.4 fusion.11
  217.6 0.9 copy-done.2
  218.5 0.3 fusion.41
  218.8 4.3 %copy.44 = bf16[320,1,32,32]{0,3,2,1:T(8,128)(2,1)} copy(bf16[320,1,32,32]{3,2,1,0:T(8,128)(2,1)S(1)} %get-tuple-element.3) | data formatting | bytes 1310720
  223.1 2.6 %fusion.12 = bf16[16,32,32]{2,0,1:T(8,128)(2,1)S(1)} fusion(bf16[320,1,32,32]{0,3,2,1:T(8,128)(2,1)} %copy.44, f32[32,16]{1,0:T(8,128)S(1)} %fusion.41, f32[32,16,320]{2,1,0:T(8,128)} %copy-done.2), kind=kOutput, calls=%fused_computation.23 | convolution fusion | flops 10994495 | bytes 1345536 | tf_op jit(solution)/shard_map/hqt,thd->qhd/dot_general | solution.py:132
  225.7 0.8 reshape.131
  (33 shorter events, 0.2 us)
Async XLA Ops:
  7.2 127.6 %copy-start = (bf16[1,1,24,8,2048]{4,3,2,1,0:T(8,128)(2,1)S(1)}, bf16[1,1,24,8,2048]{4,3,2,1,0:T(8,128)(2,1)}, u32[]{:S(2)}) copy-start(bf16[1,1,24,8,2048]{4,3,2,1,0:T(8,128)(2,1)} %param.13) | copy-start | bytes 2359300
  7.2 14.2 %slice-start = ((bf16[1,1,40,8,2048]{4,3,2,1,0:T(8,128)(2,1)}), bf16[1,1,32,8,2048]{4,3,2,1,0:T(8,128)(2,1)S(1)}, s32[]{:S(2)}) async-start(bf16[1,1,40,8,2048]{4,3,2,1,0:T(8,128)(2,1)} %param.7), calls=%async_computation.5 | async-start | bytes 2097152 | tf_op jit(solution)/shard_map/slice | solution.py:68
  7.2 121.4 %all-gather.2.cloned.1.call-start = ((), (), s32[]{:S(2)}) async-start(), calls=%async_computation.4 | async-start | bytes 8650752 | tf_op jit(solution)/shard_map/all_gather | solution.py:98
  8.6 13.4 %copy-start.7 = (pred[32]{0:T(512)(128)(4,1)}, pred[32]{0:T(512)(128)(4,1)S(1)}, u32[]{:S(2)}) copy-start(pred[32]{0:T(512)(128)(4,1)S(1)} %broadcast_compare_fusion) | copy-start | bytes 100
  10.4 11.6 %copy-start.9 = (s32[32]{0:T(128)}, s32[32]{0:T(128)S(1)}, u32[]{:S(2)}) copy-start(s32[32]{0:T(128)S(1)} %fusion.39) | copy-start | bytes 388
  11.2 18.7 %all-to-all-start = ((s32[32,1,1]{2,1,0:T(1,128)}), s32[32,1,1]{2,1,0:T(1,128)S(1)}, u32[]{:S(2)}, u32[]{:S(2)}) async-start(s32[32,1,1]{2,1,0:T(1,128)} %copy.33), calls=%async_computation | async-start | bytes 32768 | tf_op jit(solution)/shard_map/all_to_all | solution.py:80
  24.4 12.1 %copy-start.1 = (bf16[1,1,40,8,2048]{4,3,2,1,0:T(8,128)(2,1)S(1)}, bf16[1,1,40,8,2048]{4,3,2,1,0:T(8,128)(2,1)}, u32[]{:S(2)}) copy-start(bf16[1,1,40,8,2048]{4,3,2,1,0:T(8,128)(2,1)} %param.7) | copy-start | bytes 3932164
  29.9 41.5 %all-to-all-start.1 = ((bf16[32,2,8192]{2,1,0:T(2,128)(2,1)}), bf16[32,2,8192]{2,1,0:T(2,128)(2,1)}, u32[]{:S(2)}, u32[]{:S(2)}) async-start(bf16[32,2,8192]{2,1,0:T(2,128)(2,1)} %reshape.139), calls=%async_computation.1 | async-start | bytes 2097152 | tf_op jit(solution)/shard_map/all_to_all | solution.py:73
  36.5 92.1 %copy-start.3 = (bf16[8,8,2048]{2,1,0:T(8,128)(2,1)}, bf16[8,8,2048]{2,1,0:T(8,128)(2,1)S(1)}, u32[]{:S(2)}) copy-start(bf16[8,8,2048]{2,1,0:T(8,128)(2,1)S(1)} %slice_bitcast_fusion) | copy-start | bytes 786436
  75.7 52.9 %copy-start.12 = (f32[2048]{0:T(1024)S(1)}, f32[2048]{0:T(1024)}, u32[]{:S(2)}) copy-start(f32[2048]{0:T(1024)} %param.10) | copy-start | bytes 24580
  133.8 0.9 copy-start.5
  133.9 1.1 copy-start.4
  146.3 16.0 %all-to-all-start.3 = ((f32[32,1,64]{2,1,0:T(1,128)}), f32[32,1,64]{2,1,0:T(1,128)S(1)}, u32[]{:S(2)}, u32[]{:S(2)}) async-start(f32[32,1,64]{2,1,0:T(1,128)} %convolution_bitcast_fusion), calls=%async_computation.3 | async-start | bytes 32768 | tf_op jit(solution)/shard_map/all_to_all | solution.py:29
  155.6 13.0 %copy-start.6 = (bf16[1,1,16,1024]{3,2,1,0:T(8,128)(2,1)S(1)}, bf16[1,1,16,1024]{3,2,1,0:T(8,128)(2,1)}, u32[]{:S(2)}) copy-start(bf16[1,1,16,1024]{3,2,1,0:T(8,128)(2,1)} %param.12) | copy-start | bytes 98308
  155.6 13.2 %slice-start.1 = ((bf16[192,2048]{1,0:T(8,128)(2,1)}), bf16[64,2048]{1,0:T(8,128)(2,1)S(1)}, s32[]{:S(2)}) async-start(bf16[192,2048]{1,0:T(8,128)(2,1)} %copy-done.5), calls=%async_computation.6 | async-start | bytes 524288 | tf_op jit(solution)/shard_map/slice | solution.py:118
  162.2 32.7 %all-to-all-start.2 = ((bf16[32,2,8192]{2,1,0:T(2,128)(2,1)}), bf16[32,2,8192]{2,1,0:T(2,128)(2,1)}, u32[]{:S(2)}, u32[]{:S(2)}) async-start(bf16[32,2,8192]{2,1,0:T(2,128)(2,1)} %reshape.141), calls=%async_computation.2 | async-start | bytes 2097152 | tf_op jit(solution)/shard_map/all_to_all | solution.py:108
  168.8 30.4 %copy-start.8 = (pred[32]{0:T(512)(128)(4,1)S(1)}, pred[32]{0:T(512)(128)(4,1)}, u32[]{:S(2)}) copy-start(pred[32]{0:T(512)(128)(4,1)} %copy-done.7) | copy-start | bytes 100
  168.8 30.4 %copy-start.10 = (s32[32]{0:T(128)S(1)}, s32[32]{0:T(128)}, u32[]{:S(2)}) copy-start(s32[32]{0:T(128)} %copy-done.9) | copy-start | bytes 388
  211.2 5.1 %copy-start.11 = (pred[320]{0:T(512)(128)(4,1)S(1)}, pred[320]{0:T(512)(128)(4,1)}, u32[]{:S(2)}) copy-start(pred[320]{0:T(512)(128)(4,1)} %broadcast_in_dim.42) | copy-start | bytes 964
  217.6 0.9 copy-start.2
Sparse Core Ops, SparseCore 0:
  11.2 117.3 all-gather.1
where the time goes:
time: 234 us; the launch traced here: 233 us
  waiting for transfers between devices  99.4 us (42%)
  local copies, waits for them, and re-layouts  39.6 us (17%)
  starting transfers between devices  29.1 us (12%)
  matrix products  22.2 us (9%)
  blocking collectives  21.1 us (9%)
  between operations  15 us (6%)
  other arithmetic  6.97 us (3%)
    all_gather x1, waiting for transfers between devices, shards(): weight_piece = lax.all_gather(projection, 'fsdp', axis=0, tiled=True)  51 us
    all_to_all x1, waiting for transfers between devices, shards(): lax.all_to_all(outgoing.reshape(peer_count, per_peer, LEN * D), 'fsdp', s...  33.8 us
    unnamed x34, local copies, waits for them, and re-layouts  23.8 us
    psum x2, blocking collectives, by_axis(): array = lax.psum(array, axis)  21.1 us
    all_to_all x1, starting transfers between devices, shards(): lax.all_to_all(slot_tags.reshape(peer_count, per_peer), 'fsdp', split_axi...  10.2 us
    dot_general x1, matrix products, shards(): lax.dot_general(upstream, weight_piece, (((1,), (1,)), ((), ())), preferr...  7.42 us
    all_to_all x1, starting transfers between devices, sent_and_summed(): parts = lax.all_to_all(cut_along(array, dim, peers), axis, 0, 0, tiled=True)  7.39 us
    all_to_all x1, starting transfers between devices, shards(): lax.all_to_all(outgoing.reshape(peer_count, per_peer, LEN * D), 'fsdp', s...  5.87 us
  transfers between devices with their start and end apart: 5, of which 5 were waited for; matrix products, arithmetic and copies ran while one was open for 8% of the time, Pallas kernels for 0%

commit v1 on v0

--- a/solution.py
+++ b/solution.py
@@ -95,7 +95,11 @@
     )
     token_alive = jnp.repeat(slot_alive, LEN).astype(jnp.float32)
     upstream = cotangent.reshape(ENC * LEN, 2 * HW)
-    weight_piece = lax.all_gather(projection, "fsdp", axis=0, tiled=True)
+    size = lax.axis_size("fsdp")
+    repeats = [size if d == 0 else 1 for d in range(projection.ndim)]
+    weight_piece = lax.all_to_all(
+        jnp.tile(projection, repeats), "fsdp", split_axis=0, concat_axis=0, tiled=True
+    )
     partial_states = jnp.dot(scaled, weight_piece, preferred_element_type=jnp.float32)
     back_piece = lax.dot_general(
         upstream, weight_piece, (((1,), (1,)), ((), ())), preferred_element_type=jnp.float32

time: 234 us -> 354 us (1.51)
  the two profiles are of different devices: /device:TPU:8 before, /device:TPU:1 now
where the time goes in v1:
time: 354 us
  waiting for transfers between devices  185 us (52%)
  blocking collectives  57.3 us (16%)
  local copies, waits for them, and re-layouts  43.1 us (12%)
  starting transfers between devices  36.9 us (10%)
  matrix products  22.3 us (6%)
  other arithmetic  7.1 us (2%)
    all_to_all x1, waiting for transfers between devices, shards(): lax.all_to_all(jnp.tile(projection, repeats), 'fsdp', split_axis=0, conca...  175 us
    all_to_all x1, blocking collectives, shards(): lax.all_to_all(outgoing.reshape(peer_count, per_peer, LEN * D), 'fsdp', s...  29.6 us
    psum x2, blocking collectives, by_axis(): array = lax.psum(array, axis)  27.7 us
    unnamed x36, local copies, waits for them, and re-layouts  23 us
    all_to_all x1, starting transfers between devices, sent_and_summed(): parts = lax.all_to_all(cut_along(array, dim, peers), axis, 0, 0, tiled=True)  13.5 us
    all_to_all x1, starting transfers between devices, shards(): lax.all_to_all(slot_tags.reshape(peer_count, per_peer), 'fsdp', split_axi...  10.5 us
    all_to_all x1, starting transfers between devices, shards(): lax.all_to_all(jnp.tile(projection, repeats), 'fsdp', split_axis=0, conca...  8.29 us
    dot_general x1, matrix products, shards(): lax.dot_general(upstream, weight_piece, (((1,), (1,)), ((), ())), preferr...  7.52 us
  transfers between devices with their start and end apart: 4, of which 3 were waited for; matrix products, arithmetic and copies ran while one was open for 4% of the time, Pallas kernels for 0%

profile of v1, /device:TPU:1, one launch (start us, length us, event | category | flops | bytes accessed | tf_op | source)
XLA Modules:
  0.0 353.5 jit_solution(9800931553585825884)
XLA Ops:
  0.6 0.0 copy-start
  0.6 0.0 slice-start
  0.7 0.8 broadcast_compare_fusion
  1.5 0.8 add_bitcast_fusion.1
  2.2 0.1 fusion.30
  2.3 0.1 reduce_window_sum.11
  2.4 0.2 select_reduce_fusion.1
  2.5 0.7 fusion.40
  3.2 0.1 select_reduce_fusion
  3.4 0.7 copy.33
  4.1 10.5 %all-to-all-start = ((s32[32,1,1]{2,1,0:T(1,128)}), s32[32,1,1]{2,1,0:T(1,128)S(1)}, u32[]{:S(2)}, u32[]{:S(2)}) async-start(s32[32,1,1]{2,1,0:T(1,128)} %copy.33), calls=%async_computation | async-start | bytes 32768 | tf_op jit(solution)/shard_map/all_to_all | solution.py:80
  14.6 0.6 copy.46
  15.2 0.4 fusion.1
  15.6 0.5 broadcast.102
  16.1 1.4 reduce.2
  17.6 0.0 copy-start.6
  17.6 0.8 reshape.193
  18.4 4.8 %all-to-all-done = s32[32,1,1]{2,1,0:T(1,128)S(1)} async-done(((s32[32,1,1]{2,1,0:T(1,128)}), s32[32,1,1]{2,1,0:T(1,128)S(1)}, u32[]{:S(2)}, u32[]{:S(2)}) %all-to-all-start) | async-done | bytes 160 | tf_op jit(solution)/shard_map/all_to_all | solution.py:80
  23.2 29.6 %all_to_all.34 = bf16[32,2,8192]{2,1,0:T(2,128)(2,1)} all-to-all(bf16[32,2,8192]{2,1,0:T(2,128)(2,1)S(1)} %reshape.193), channel_id=1, replica_groups=mesh['dp_0'=8,'dp_1'=2,'fsdp'=32] {'fsdp'}, dimensions={0} | all-to-all | bytes 2097152 | tf_op jit(solution)/shard_map/all_to_all | solution.py:73
  52.7 4.3 %tile.2 = bf16[32,64,2048]{2,1,0:T(8,128)(2,1)} broadcast(bf16[64,2048]{1,0:T(8,128)(2,1)S(1)} %copy-done.6), dimensions={1,2} | broadcast | bytes 8650752 | tf_op jit(solution)/shard_map/tile | solution.py:101
  57.0 8.3 %all-to-all-start.2 = ((bf16[32,64,2048]{2,1,0:T(8,128)(2,1)}), bf16[32,64,2048]{2,1,0:T(8,128)(2,1)}, u32[]{:S(2)}, u32[]{:S(2)}) async-start(bf16[32,64,2048]{2,1,0:T(8,128)(2,1)} %tile.2), calls=%async_computation.2 | async-start | bytes 16777216 | tf_op jit(solution)/shard_map/all_to_all | solution.py:100
  66.0 0.7 reduce.1
  66.7 0.1 fusion.31
  66.8 0.1 pad_add_fusion
  66.9 0.1 broadcast_in_dim.45
  66.9 0.1 reshape.189
  67.0 4.3 %reshape.194 = bf16[32,1,16384]{2,1,0:T(2,128)(2,1)S(1)} reshape(bf16[32,2,8192]{2,1,0:T(2,128)(2,1)} %all_to_all.34) | data formatting | bytes 2097152
  71.4 1.2 convolution_convert_fusion.3
  72.6 0.3 copy.47
  72.9 0.2 fusion.4
  73.1 0.1 rsqrt.13
  73.2 175.4 %all-to-all-done.2 = bf16[32,64,2048]{2,1,0:T(8,128)(2,1)} async-done(((bf16[32,64,2048]{2,1,0:T(8,128)(2,1)}), bf16[32,64,2048]{2,1,0:T(8,128)(2,1)}, u32[]{:S(2)}, u32[]{:S(2)}) %all-to-all-start.2) | async-done | bytes 8388640 | tf_op jit(solution)/shard_map/all_to_all | solution.py:100
  248.6 5.2 %convolution_convert_fusion.4 = bf16[192,2048]{1,0:T(8,128)(2,1)S(1)} fusion(bf16[2048,2048]{1,0:T(8,128)(2,1)} %bitcast.6, f32[2048]{0:T(1024)S(1)} %copy-done.13, f32[24,8]{1,0:T(8,128)S(1)} %add_rsqrt_fusion, bf16[16,8,2048]{2,1,0:T(8,128)(2,1)S(1)} %bitcast.74, bf16[8,8,2048]{2,1,0:T(8,128)(2,1)S(1)} %slice_bitcast_fusion), kind=kOutput, calls=%fused_computation.9 | convolution fusion | flops 1612972032 | bytes 9970432 | tf_op jit(solution)/shard_map/dot_general | solution.py:103
  253.9 0.2 slice.45
  254.2 0.6 copy-done.5
  254.8 0.3 copy-done.4
  255.0 7.5 %fusion.3 = f32[2048,192]{0,1:T(8,128)} fusion(bf16[2048,2048]{1,0:T(8,128)(2,1)} %bitcast.6, bf16[1,1,24,8,2048]{4,3,2,1,0:T(8,128)(2,1)S(1)} %copy-done, f32[192]{0:T(256)S(1)} %rsqrt.13, bf16[16,8,2048]{2,1,0:T(8,128)(2,1)S(1)} %bitcast.75, bf16[8,8,2048]{2,1,0:T(8,128)(2,1)S(1)} %copy-done.4), kind=kOutput, calls=%fused_computation.8 | convolution fusion | flops 1612185600 | bytes 11535104 | tf_op jit(solution)/shard_map/dot_general | solution.py:104
  262.5 1.8 copy.40
  264.4 2.0 convolution_bitcast_fusion
  266.4 13.5 %all-to-all-start.4 = ((f32[32,1,64]{2,1,0:T(1,128)}), f32[32,1,64]{2,1,0:T(1,128)S(1)}, u32[]{:S(2)}, u32[]{:S(2)}) async-start(f32[32,1,64]{2,1,0:T(1,128)} %convolution_bitcast_fusion), calls=%async_computation.4 | async-start | bytes 32768 | tf_op jit(solution)/shard_map/all_to_all | solution.py:29
  279.9 0.5 fusion.2
  280.3 1.4 reduce.3
  281.8 1.6 reshape.195
  283.4 5.0 %all-to-all-done.4 = f32[32,1,64]{2,1,0:T(1,128)S(1)} async-done(((f32[32,1,64]{2,1,0:T(1,128)}), f32[32,1,64]{2,1,0:T(1,128)S(1)}, u32[]{:S(2)}, u32[]{:S(2)}) %all-to-all-start.4) | async-done | bytes 8224 | tf_op jit(solution)/shard_map/all_to_all | solution.py:29
  288.5 4.7 %all-to-all-start.3 = ((bf16[32,2,8192]{2,1,0:T(2,128)(2,1)}), bf16[32,2,8192]{2,1,0:T(2,128)(2,1)}, u32[]{:S(2)}, u32[]{:S(2)}) async-start(bf16[32,2,8192]{2,1,0:T(2,128)(2,1)} %reshape.195), calls=%async_computation.3 | async-start | bytes 2097152 | tf_op jit(solution)/shard_map/all_to_all | solution.py:112
  293.1 0.1 broadcast_in_dim.41
  293.2 0.6 broadcast_in_dim.42
  293.8 0.1 reshape.184
  294.0 0.1 slice.43
  294.1 0.1 reduce_sum.49
  294.2 21.0 %psum.14 = f32[64]{0:T(128)S(1)} all-reduce(f32[64]{0:T(128)S(1)} %reduce_sum.49), channel_id=1, replica_groups=mesh['dp_0'=8,'dp_1'=2,'fsdp'=32] {'dp_0'}, use_global_device_ids=true, to_apply=%region_8.9 | all-reduce | flops 64 | bytes 512 | tf_op jit(solution)/shard_map/psum | solution.py:35
  315.2 6.7 %psum.15 = f32[64]{0:T(128)} all-reduce(f32[64]{0:T(128)S(1)} %psum.14), channel_id=1, replica_groups=mesh['dp_0'=8,'dp_1'=2,'fsdp'=32] {'dp_1'}, use_global_device_ids=true, to_apply=%region_9.10 | all-reduce | flops 64 | bytes 512 | tf_op jit(solution)/shard_map/psum | solution.py:35
  321.9 4.3 %reshape.196 = bf16[32,1,16384]{2,1,0:T(2,128)(2,1)S(1)} reshape(bf16[32,2,8192]{2,1,0:T(2,128)(2,1)} %all-to-all-done.3) | data formatting | bytes 2097152
  326.2 1.4 convolution_convert_fusion
  327.7 0.1 pad_maximum_fusion
  327.8 5.4 %reshape.182 = bf16[320,2,32,32]{3,2,1,0:T(8,128)(2,1)} reshape(bf16[40,16384]{1,0:T(8,128)(2,1)S(1)} %pad_maximum_fusion) | data formatting | bytes 2621440 | tf_op jit(solution)/shard_map/reshape | solution.py:122
  333.2 5.0 %fusion.41 = (bf16[320,1,32,32]{3,2,1,0:T(8,128)(2,1)}, bf16[320,1,32,32]{3,2,1,0:T(8,128)(2,1)S(1)}) fusion(bf16[320,2,32,32]{3,2,1,0:T(8,128)(2,1)} %reshape.182), kind=kLoop, calls=%fused_computation.67 | loop fusion | bytes 2621440 | tf_op jit(solution)/shard_map/slice | solution.py:125
  338.2 5.1 %copy.45 = bf16[320,1,32,32]{0,3,2,1:T(8,128)(2,1)} copy(bf16[320,1,32,32]{3,2,1,0:T(8,128)(2,1)} %get-tuple-element.2) | data formatting | bytes 1310720
  343.2 1.4 fusion.11
  344.7 0.9 copy-done.2
  345.6 0.3 fusion.42
  345.8 4.3 %copy.44 = bf16[320,1,32,32]{0,3,2,1:T(8,128)(2,1)} copy(bf16[320,1,32,32]{3,2,1,0:T(8,128)(2,1)S(1)} %get-tuple-element.3) | data formatting | bytes 1310720
  350.1 2.6 fusion.12
  352.7 0.8 reshape.185
  (34 shorter events, 0.2 us)
Async XLA Ops:
  0.6 254.1 %copy-start = (bf16[1,1,24,8,2048]{4,3,2,1,0:T(8,128)(2,1)S(1)}, bf16[1,1,24,8,2048]{4,3,2,1,0:T(8,128)(2,1)}, u32[]{:S(2)}) copy-start(bf16[1,1,24,8,2048]{4,3,2,1,0:T(8,128)(2,1)} %param.13) | copy-start | bytes 2359300
  0.6 13.9 %slice-start = ((bf16[1,1,40,8,2048]{4,3,2,1,0:T(8,128)(2,1)}), bf16[1,1,32,8,2048]{4,3,2,1,0:T(8,128)(2,1)S(1)}, s32[]{:S(2)}) async-start(bf16[1,1,40,8,2048]{4,3,2,1,0:T(8,128)(2,1)} %param.7), calls=%async_computation.5 | async-start | bytes 2097152 | tf_op jit(solution)/shard_map/slice | solution.py:68
  1.5 13.7 %copy-start.8 = (pred[32]{0:T(512)(128)(4,1)}, pred[32]{0:T(512)(128)(4,1)S(1)}, u32[]{:S(2)}) copy-start(pred[32]{0:T(512)(128)(4,1)S(1)} %broadcast_compare_fusion) | copy-start | bytes 100
  3.2 11.9 %copy-start.10 = (s32[32]{0:T(128)}, s32[32]{0:T(128)S(1)}, u32[]{:S(2)}) copy-start(s32[32]{0:T(128)S(1)} %fusion.40) | copy-start | bytes 388
  4.1 19.1 %all-to-all-start = ((s32[32,1,1]{2,1,0:T(1,128)}), s32[32,1,1]{2,1,0:T(1,128)S(1)}, u32[]{:S(2)}, u32[]{:S(2)}) async-start(s32[32,1,1]{2,1,0:T(1,128)} %copy.33), calls=%async_computation | async-start | bytes 32768 | tf_op jit(solution)/shard_map/all_to_all | solution.py:80
  17.6 35.1 %copy-start.6 = (bf16[64,2048]{1,0:T(8,128)(2,1)S(1)}, bf16[64,2048]{1,0:T(8,128)(2,1)}, u32[]{:S(2)}) copy-start(bf16[64,2048]{1,0:T(8,128)(2,1)} %param.11) | copy-start | bytes 786436
  57.0 9.0 %copy-start.1 = (bf16[1,1,40,8,2048]{4,3,2,1,0:T(8,128)(2,1)S(1)}, bf16[1,1,40,8,2048]{4,3,2,1,0:T(8,128)(2,1)}, u32[]{:S(2)}) copy-start(bf16[1,1,40,8,2048]{4,3,2,1,0:T(8,128)(2,1)} %param.7) | copy-start | bytes 3932164
  57.0 191.6 %all-to-all-start.2 = ((bf16[32,64,2048]{2,1,0:T(8,128)(2,1)}), bf16[32,64,2048]{2,1,0:T(8,128)(2,1)}, u32[]{:S(2)}, u32[]{:S(2)}) async-start(bf16[32,64,2048]{2,1,0:T(8,128)(2,1)} %tile.2), calls=%async_computation.2 | async-start | bytes 16777216 | tf_op jit(solution)/shard_map/all_to_all | solution.py:100
  66.0 182.6 %copy-start.3 = (bf16[8,8,2048]{2,1,0:T(8,128)(2,1)}, bf16[8,8,2048]{2,1,0:T(8,128)(2,1)S(1)}, u32[]{:S(2)}) copy-start(bf16[8,8,2048]{2,1,0:T(8,128)(2,1)S(1)} %slice_bitcast_fusion) | copy-start | bytes 786436
  71.4 177.3 %copy-start.13 = (f32[2048]{0:T(1024)S(1)}, f32[2048]{0:T(1024)}, u32[]{:S(2)}) copy-start(f32[2048]{0:T(1024)} %param.10) | copy-start | bytes 24580
  253.9 0.9 copy-start.5
  253.9 1.1 copy-start.4
  266.4 22.1 %all-to-all-start.4 = ((f32[32,1,64]{2,1,0:T(1,128)}), f32[32,1,64]{2,1,0:T(1,128)S(1)}, u32[]{:S(2)}, u32[]{:S(2)}) async-start(f32[32,1,64]{2,1,0:T(1,128)} %convolution_bitcast_fusion), calls=%async_computation.4 | async-start | bytes 32768 | tf_op jit(solution)/shard_map/all_to_all | solution.py:29
  281.8 12.0 %copy-start.7 = (bf16[1,1,16,1024]{3,2,1,0:T(8,128)(2,1)S(1)}, bf16[1,1,16,1024]{3,2,1,0:T(8,128)(2,1)}, u32[]{:S(2)}) copy-start(bf16[1,1,16,1024]{3,2,1,0:T(8,128)(2,1)} %param.12) | copy-start | bytes 98308
  281.8 12.2 %slice-start.1 = ((bf16[192,2048]{1,0:T(8,128)(2,1)}), bf16[64,2048]{1,0:T(8,128)(2,1)S(1)}, s32[]{:S(2)}) async-start(bf16[192,2048]{1,0:T(8,128)(2,1)} %copy-done.5), calls=%async_computation.6 | async-start | bytes 524288 | tf_op jit(solution)/shard_map/slice | solution.py:122
  288.5 33.5 %all-to-all-start.3 = ((bf16[32,2,8192]{2,1,0:T(2,128)(2,1)}), bf16[32,2,8192]{2,1,0:T(2,128)(2,1)}, u32[]{:S(2)}, u32[]{:S(2)}) async-start(bf16[32,2,8192]{2,1,0:T(2,128)(2,1)} %reshape.195), calls=%async_computation.3 | async-start | bytes 2097152 | tf_op jit(solution)/shard_map/all_to_all | solution.py:112
  294.0 32.2 %copy-start.9 = (pred[32]{0:T(512)(128)(4,1)S(1)}, pred[32]{0:T(512)(128)(4,1)}, u32[]{:S(2)}) copy-start(pred[32]{0:T(512)(128)(4,1)} %copy-done.8) | copy-start | bytes 100
  294.0 32.2 %copy-start.11 = (s32[32]{0:T(128)S(1)}, s32[32]{0:T(128)}, u32[]{:S(2)}) copy-start(s32[32]{0:T(128)} %copy-done.10) | copy-start | bytes 388
  338.2 5.1 %copy-start.12 = (pred[320]{0:T(512)(128)(4,1)S(1)}, pred[320]{0:T(512)(128)(4,1)}, u32[]{:S(2)}) copy-start(pred[320]{0:T(512)(128)(4,1)} %broadcast_in_dim.42) | copy-start | bytes 964
  344.6 0.9 copy-start.2
